TPU v7x, 32 devices: a whole 2x2x4 slice. The times are simulated.
32 devices in a mesh: seq: 4 (over x, core), head: 8 (over z, y).
Axes of the slice: x: 2, y: 2, z: 4, core: 2. Of those that a mesh axis runs over, the one named last changes fastest.
Arguments:
- queries: bfloat16 [256, 4096], P('seq', 'head'), may hold values from -8 to 8
- new_keys: bfloat16 [256, 256], P('seq'), may hold values from -6 to 6
- new_values: bfloat16 [256, 256], P('seq'), may hold values from -6 to 6
- cache_keys: bfloat16 [3072, 256], P('seq'), may hold values from -8 to 8
- cache_values: bfloat16 [3072, 256], P('seq'), may hold values from -6 to 6
- positions: int32 [256], replicated, may hold values from 0 to 255, each once
- cache_len: int32 [4], replicated, may hold values from 1 to 768, 1920 in all
- out_weight: bfloat16 [4096, 16384], P('head', 'seq'), may hold values from -3.5 to 3.5
Outputs:
- output: float32 [256, 16384], P(None, 'seq')
Inputs may be any that keep to these rules, and one draw needn't show every extreme that they name: A permutation of the block's positions 0 to 255. `cache_len`: entry s is the number of live slots at the start of sequence group s's 768 cache slots; later slots of that group are not attended. Some group is full.
All inputs are finite; a program needn't handle non-finite values.
Results may differ from a plain program's by a relative error of at most 0.009.
Values may be sent and summed in bfloat16 or wider, within the bound.
A program may use at most 128 MiB of HBM per device.

v0:
```python
from functools import partial
import jax
import jax.numpy as jnp
from jax import lax
from jax.sharding import PartitionSpec as P

DH = 128
GQA = 16


def key_mask(count, query_pos, positions, cache_len, stripe, tok_dev):
    index = jnp.arange(count, dtype=jnp.int32)
    span = stripe + tok_dev
    group = index // span
    offset = index % span
    groups = jnp.arange(cache_len.shape[0], dtype=jnp.int32)
    live_len = jnp.sum(jnp.where(group[:, None] == groups[None, :], cache_len[None, :], 0), axis=1)
    is_cache = offset < stripe
    token = jnp.clip(group * tok_dev + offset - stripe, 0, positions.shape[0] - 1)
    key_pos = jnp.take(positions, token)
    return jnp.where(
        is_cache[None, :], (offset < live_len)[None, :], key_pos[None, :] <= query_pos[:, None]
    )


def softmax_step(
    state, block, begin, query_heads, query_pos, positions, cache_len, stripe, tok_dev
):
    running_max, running_sum, weighted = state
    keys = block[:, :DH]
    values = block[:, DH:]
    scores = jnp.einsum(
        "thd,kd->thk", query_heads, keys, preferred_element_type=jnp.float32
    ) * DH ** (-0.5)
    shown = key_mask(block.shape[0], query_pos, positions, cache_len, stripe, tok_dev)[:, None, :]
    scores = jnp.where(shown, scores, -1e30)
    new_max = jnp.maximum(running_max, jnp.max(scores, axis=2))
    expo = jnp.where(shown, jnp.exp(scores - new_max[:, :, None]), 0.0)
    running_sum = jnp.sum(expo, axis=2)
    weighted = jnp.einsum(
        "thk,kd->thd", expo.astype(jnp.bfloat16), values, preferred_element_type=jnp.float32
    )
    return (new_max, running_sum, weighted)


def empty_state(rows, heads_dev):
    return (
        jnp.full((rows, heads_dev), -1e30, jnp.float32),
        jnp.zeros((rows, heads_dev), jnp.float32),
        jnp.zeros((rows, heads_dev, DH), jnp.float32),
    )


def body(queries, new_keys, new_values, cache_keys, cache_values, positions, cache_len, out_weight):
    tok_dev = queries.shape[0]
    heads_dev = queries.shape[1] // DH
    stripe = cache_keys.shape[0]
    seq_index = lax.axis_index("seq")
    head_index = lax.axis_index("head")
    column = head_index * heads_dev // GQA * DH
    own_keys = jnp.concatenate(
        [
            lax.dynamic_slice_in_dim(cache_keys, column, DH, 1),
            lax.dynamic_slice_in_dim(new_keys, column, DH, 1),
        ],
        axis=0,
    )
    own_values = jnp.concatenate(
        [
            lax.dynamic_slice_in_dim(cache_values, column, DH, 1),
            lax.dynamic_slice_in_dim(new_values, column, DH, 1),
        ],
        axis=0,
    )
    key_block = jnp.concatenate([own_keys, own_values], axis=1)
    query_heads = queries.reshape(tok_dev, heads_dev, DH)
    query_pos = lax.dynamic_slice_in_dim(positions, seq_index * tok_dev, tok_dev)
    stepper = partial(
        softmax_step,
        query_heads=query_heads,
        query_pos=query_pos,
        positions=positions,
        cache_len=cache_len,
        stripe=stripe,
        tok_dev=tok_dev,
    )
    final_max, final_sum, weighted = stepper(
        empty_state(tok_dev, heads_dev),
        lax.all_gather(key_block, "seq", axis=0, tiled=True),
        jnp.int32(0),
    )
    attended = (
        (weighted / final_sum[:, :, None]).astype(jnp.bfloat16).reshape(tok_dev, heads_dev * DH)
    )
    partial_out = jnp.dot(
        lax.all_gather(attended, "seq", axis=0, tiled=True),
        out_weight,
        preferred_element_type=jnp.float32,
    )
    return lax.psum(partial_out, "head")


def solution(mesh):
    placed = (
        P("seq", "head"),
        P("seq", None),
        P("seq", None),
        P("seq", None),
        P("seq", None),
        P(),
        P(),
        P("head", "seq"),
    )
    return jax.shard_map(
        body, mesh=mesh, in_specs=placed, out_specs=P(None, "seq"), check_vma=False
    )
```

profile of v0, /device:TPU:0, one launch (start us, length us, event | category | flops | bytes accessed | tf_op | source)
XLA Modules:
  0.0 214.3 jit_solution(2551049296829856070)
XLA Ops:
  6.5 0.0 copy-start
  6.5 0.0 copy-start.1
  6.5 0.0 all-gather.2.cloned.1.call-start
  6.5 0.8 constant_dynamic-slice_fusion
  7.3 1.0 constant_dynamic-slice_fusion.1
  8.4 0.8 maximum_maximum_fusion
  9.2 0.0 all-gather.2.cloned.1.call-update
  9.2 0.0 all-reduce.2.cloned.1.call-start
  9.3 0.8 dynamic_slice.15
  10.0 0.1 fusion.28
  10.1 0.0 copy-done.1
  10.2 0.0 copy-start.3
  10.2 19.9 %gather_fusion = s32[3328]{0:T(1024)S(1)} fusion(s32[256]{0:T(256)S(1)} %copy-done.1, s32[4096]{0:T(1024)S(1)} %pad_clamp_fusion), kind=kCustom, calls=%fused_computation | custom fusion | bytes 39936 | tf_op jit(solution)/shard_map/jit(_take)/gather | solution.py:20
  30.1 0.0 copy-done.3
  30.1 0.1 select_reduce_fusion
  30.3 0.2 compare_select_fusion
  30.5 2.0 all-gather.2.cloned.1.call-done
  32.4 0.0 copy-done
  32.4 0.0 copy-start.4
  32.5 2.2 %fusion.33 = (f32[64,4]{0,1:T(4,128)S(1)}, f32[64,4,3328]{2,0,1:T(8,128)S(1)}) fusion(bf16[3328,256]{1,0:T(8,128)(2,1)} %all-gather.2.cloned.1.call-done, pred[64,3328]{1,0:T(8,128)(4,1)S(1)} %compare_select_fusion, bf16[64,512]{1,0:T(8,128)(2,1)S(1)} %copy-done), kind=kOutput, calls=%fused_computation.55 | convolution fusion | flops 220659456 | bytes 4539392 | tf_op jit(solution)/shard_map/thd,kd->thk/dot_general | solution.py:32
  34.6 0.8 fusion.2
  35.5 0.0 copy-done.4
  35.5 0.0 copy-start.2
  35.5 0.8 fusion.15
  36.3 5.9 %all_gather.7 = bf16[256,512]{1,0:T(8,128)(2,1)S(1)} all-gather(bf16[64,512]{1,0:T(8,128)(2,1)S(1)} %bitcast.28), channel_id=1, replica_groups=mesh['seq'=4,'head'=8] {'seq'}, dimensions={0}, use_global_device_ids=true | all-gather | bytes 327680 | tf_op jit(solution)/shard_map/all_gather | solution.py:96
  42.2 0.0 copy-done.2
  42.2 3.3 %fusion.34 = f32[256,4096]{1,0:T(8,128)} fusion(bf16[256,512]{1,0:T(8,128)(2,1)S(1)} %all_gather.7, bf16[512,4096]{1,0:T(8,128)(2,1)S(1)} %copy-done.2), kind=kOutput, calls=%fused_computation.56 | convolution fusion | flops 1073741824 | bytes 8650752 | tf_op jit(solution)/shard_map/dot_general | solution.py:95
  45.5 0.0 all-reduce.2.cloned.1.call-update
  45.5 157.3 %all-reduce.2.cloned.1.call-done = f32[256,4096]{1,0:T(8,128)} async-done(((f32[256,4096]{1,0:T(8,128)}), f32[256,4096]{1,0:T(8,128)}) %all-reduce.2.cloned.1.call-update) | async-done | bytes 4194320 | tf_op jit(solution)/shard_map/psum | solution.py:100
  202.8 4.7 %copy.25 = f32[256,4096]{1,0:T(8,128)} copy(f32[256,4096]{1,0:T(8,128)} %all-reduce.2.cloned.1.call-done) | data formatting | bytes 8388608
  (6 shorter events, 0.1 us)
Async XLA Ops:
  6.5 25.9 %copy-start = (bf16[64,512]{1,0:T(8,128)(2,1)S(1)}, bf16[64,512]{1,0:T(8,128)(2,1)}, u32[]{:S(2)}) copy-start(bf16[64,512]{1,0:T(8,128)(2,1)} %param.8) | copy-start | bytes 196612
  6.5 3.6 %copy-start.1 = (s32[256]{0:T(256)S(1)}, s32[256]{0:T(256)}, u32[]{:S(2)}) copy-start(s32[256]{0:T(256)} %param.13) | copy-start | bytes 3076
  6.5 25.9 %all-gather.2.cloned.1.call-start = ((), (), s32[]{:S(2)}) async-start(), calls=%async_computation | async-start | bytes 2129920 | tf_op jit(solution)/shard_map/all_gather | solution.py:89
  9.2 193.6 %all-reduce.2.cloned.1.call-start = ((), (), s32[]{:S(2)}) async-start(), calls=%async_computation.1 | async-start | bytes 8388608 | tf_op jit(solution)/shard_map/psum | solution.py:100
  10.2 19.9 %copy-start.3 = (s32[4]{0:T(128)S(1)}, s32[4]{0:T(128)}, u32[]{:S(2)}) copy-start(s32[4]{0:T(128)} %param.14) | copy-start | bytes 52
  32.4 3.0 %copy-start.4 = (bf16[3328,256]{1,0:T(8,128)(2,1)S(1)}, bf16[3328,256]{1,0:T(8,128)(2,1)}, u32[]{:S(2)}) copy-start(bf16[3328,256]{1,0:T(8,128)(2,1)} %all-gather.2.cloned.1.call-done) | copy-start | bytes 5111812
  35.5 6.8 %copy-start.2 = (bf16[512,4096]{1,0:T(8,128)(2,1)S(1)}, bf16[512,4096]{1,0:T(8,128)(2,1)}, u32[]{:S(2)}) copy-start(bf16[512,4096]{1,0:T(8,128)(2,1)} %param.15) | copy-start | bytes 12582916
Sparse Core Ops, SparseCore 0:
  9.3 23.0 all-gather.1
  45.7 157.1 all-reduce.1
where the time goes:
time: 215 us; the launch traced here: 214 us
  waiting for transfers between devices  159 us (74%)
  local copies, waits for them, and re-layouts  27.2 us (13%)
  between operations  13.5 us (6%)
  matrix products  6.27 us (3%)
  blocking collectives  5.91 us (3%)
  other arithmetic  2.15 us (1%)
    psum x1, waiting for transfers between devices, body(): return lax.psum(partial_out, 'head')  157 us
    gather x1, local copies, waits for them, and re-layouts, key_mask(): key_pos = jnp.take(positions, token)  19.9 us
    all_gather x1, blocking collectives, body(): lax.all_gather(attended, 'seq', axis=0, tiled=True)  5.91 us
    unnamed x11, local copies, waits for them, and re-layouts  4.67 us
  transfers between devices with their start and end apart: 2, of which 2 were waited for; matrix products, arithmetic and copies ran while one was open for 10% of the time, Pallas kernels for 0%

commit v1 on v0

--- a/solution.py
+++ b/solution.py
@@ -97,7 +97,7 @@
         out_weight,
         preferred_element_type=jnp.float32,
     )
-    return lax.psum(partial_out, "head")
+    return jnp.sum(lax.all_gather(partial_out, "head"), axis=0)
 
 
 def solution(mesh):

time: 215 us -> 705 us (3.28)
  waiting for transfers between devices: 159 us -> 641 us
  other arithmetic: 2.15 us -> 16.2 us
    all_gather x0 -> x1, waiting for transfers between devices: none -> 639 us  [body(): return jnp.sum(lax.all_gather(partial_out, 'head'), axis=0)]
    psum x1 -> x0, waiting for transfers between devices: 157 us -> none  [body(): return lax.psum(partial_out, 'head')]
    reduce_sum x0 -> x1, other arithmetic: none -> 14 us  [body(): return jnp.sum(lax.all_gather(partial_out, 'head'), axis=0)]
  transfers between devices with their start and end apart: 2 -> 2, of which waited for: 2 -> 2; matrix products, arithmetic and copies ran while one was open for 10% -> 3% of each run, Pallas kernels for 0% -> 0%
where the time goes in v1:
time: 705 us
  waiting for transfers between devices  641 us (91%)
  local copies, waits for them, and re-layouts  22.5 us (3%)
  other arithmetic  16.2 us (2%)
  between operations  13.5 us (2%)
    all_gather x1, waiting for transfers between devices, body(): return jnp.sum(lax.all_gather(partial_out, 'head'), axis=0)  639 us
    gather x1, local copies, waits for them, and re-layouts, key_mask(): key_pos = jnp.take(positions, token)  19.9 us
  transfers between devices with their start and end apart: 2, of which 2 were waited for; matrix products, arithmetic and copies ran while one was open for 3% of the time, Pallas kernels for 0%

profile of v1, /device:TPU:0, one launch (start us, length us, event | category | flops | bytes accessed | tf_op | source)
XLA Modules:
  0.0 705.0 jit_solution(14442013560388513237)
XLA Ops:
  6.5 0.0 copy-start
  6.5 0.0 copy-start.1
  6.5 0.0 all-gather.4.cloned.1.call-start
  6.5 0.8 constant_dynamic-slice_fusion
  7.3 1.0 constant_dynamic-slice_fusion.1
  8.4 0.8 maximum_maximum_fusion
  9.2 0.0 all-gather.4.cloned.1.call-update
  9.2 0.0 all-gather.6.cloned.1.call-start
  9.3 0.8 dynamic_slice.15
  10.0 0.1 fusion.28
  10.1 0.0 copy-done.1
  10.2 0.0 copy-start.3
  10.2 19.9 %gather_fusion = s32[3328]{0:T(1024)S(1)} fusion(s32[256]{0:T(256)S(1)} %copy-done.1, s32[4096]{0:T(1024)S(1)} %pad_clamp_fusion), kind=kCustom, calls=%fused_computation | custom fusion | bytes 39936 | tf_op jit(solution)/shard_map/jit(_take)/gather | solution.py:20
  30.1 0.0 copy-done.3
  30.1 0.1 select_reduce_fusion
  30.3 0.2 compare_select_fusion
  30.5 2.0 all-gather.4.cloned.1.call-done
  32.4 0.0 copy-done
  32.4 0.0 copy-start.4
  32.5 2.2 fusion.33
  34.6 0.8 fusion.2
  35.5 0.0 copy-done.4
  35.5 0.0 copy-start.2
  35.5 0.8 fusion.15
  36.3 5.9 all_gather.13
  42.2 0.0 copy-done.2
  42.2 3.3 fusion.34
  45.5 0.0 all-gather.6.cloned.1.call-update
  45.5 638.6 %all-gather.6.cloned.1.call-done = f32[2048,4096]{1,0:T(8,128)} async-done(((f32[256,4096]{1,0:T(8,128)}), f32[2048,4096]{1,0:T(8,128)}) %all-gather.6.cloned.1.call-update) | async-done | bytes 33554448 | tf_op jit(solution)/shard_map/all_gather | solution.py:100
  684.1 14.0 %reduce_sum.29 = f32[256,4096]{1,0:T(8,128)} reduce(f32[8,256,4096]{2,1,0:T(8,128)} %bitcast.29, f32[]{:T(128)} %constant.77.clone.1), dimensions={0}, to_apply=%region_3.4 | reduce | flops 7340032 | bytes 37748740 | tf_op jit(solution)/shard_map/reduce_sum | solution.py:100
  (6 shorter events, 0.1 us)
Async XLA Ops:
  6.5 25.9 %copy-start = (bf16[64,512]{1,0:T(8,128)(2,1)S(1)}, bf16[64,512]{1,0:T(8,128)(2,1)}, u32[]{:S(2)}) copy-start(bf16[64,512]{1,0:T(8,128)(2,1)} %param.8) | copy-start | bytes 196612
  6.5 3.6 copy-start.1
  6.5 25.9 %all-gather.4.cloned.1.call-start = ((), (), s32[]{:S(2)}) async-start(), calls=%async_computation | async-start | bytes 2129920 | tf_op jit(solution)/shard_map/all_gather | solution.py:89
  9.2 674.9 %all-gather.6.cloned.1.call-start = ((), (), s32[]{:S(2)}) async-start(), calls=%async_computation.1 | async-start | bytes 37748736 | tf_op jit(solution)/shard_map/all_gather | solution.py:100
  10.2 19.9 %copy-start.3 = (s32[4]{0:T(128)S(1)}, s32[4]{0:T(128)}, u32[]{:S(2)}) copy-start(s32[4]{0:T(128)} %param.14) | copy-start | bytes 52
  32.4 3.0 copy-start.4
  35.5 6.8 copy-start.2
Sparse Core Ops, SparseCore 0:
  9.3 23.0 all-gather.3
  45.7 638.4 all-gather.5
